TPU v7x, 32 devices: a whole 2x2x4 slice. The times are simulated.
32 devices in a mesh: seq: 8 (over z, x), head: 4 (over y, core).
Axes of the slice: x: 2, y: 2, z: 4, core: 2. Of those that a mesh axis runs over, the one named last changes fastest.
Arguments:
- tokens: bfloat16 [2048, 4608], P('seq', 'head'), may hold values from -32 to 32
- segments: int32 [2048], P('seq'), may hold values from 0 to 7, never falling along the last dimension, each value on 1 to 1024 neighbouring positions
- pre_gain: float32 [4608], replicated, may hold values from 0.1 to 1.9
- post_gain: float32 [4608], replicated, may hold values from 0.1 to 1.9
- w_query: bfloat16 [4608, 1024], P('seq', 'head'), may hold values from -0.375 to 0.375
- w_key: bfloat16 [4608, 512], P('seq', 'head'), may hold values from -0.1875 to 0.1875
- w_value: bfloat16 [4608, 512], P('seq', 'head'), may hold values from -0.09375 to 0.09375
- w_out: bfloat16 [1024, 4608], P('head', 'seq'), may hold values from -0.1875 to 0.1875
Outputs:
- mixed: bfloat16 [2048, 4608], P('seq')
Inputs may be any that keep to these rules, and one draw needn't show every extreme that they name: `segments`: segment ids never fall; each of the 8 documents holds at least one token and at most 1024, one exactly 1024.
All inputs are finite; a program needn't handle non-finite values.
Results may differ from a plain program's by a relative error of at most 0.01.
Values may be sent and summed in bfloat16 or wider, within the bound.
A program may use at most 64 MiB of HBM per device.

v0:
```python
import jax
import jax.numpy as jnp
from jax import lax
from jax.sharding import PartitionSpec as P

HD = 128
GROUP = 2
SCALAR = 144
DOCS = 8


EPS = 1e-06
CAP = 50.0


def carried_in(value, axis, join, neutral):
    count, mine = (lax.axis_size(axis), lax.axis_index(axis))
    pieces = lax.all_gather(value, axis)
    subtotal = jnp.full_like(value, 0) + jnp.asarray(neutral, value.dtype)

    def step(position, subtotal):
        longer = join(subtotal, pieces[position])
        return jnp.where(position < mine, longer, subtotal)

    return lax.fori_loop(0, count - 1, step, subtotal)


def rotate(values, position, width):
    count = values.shape[1] // width
    half = width // 2
    shaped = values.reshape(values.shape[0], count, width)
    freq = 10000.0 ** (-(jnp.arange(half, dtype=jnp.float32) / half))
    angle = position[:, None] * freq[None, :]
    cosine = jnp.cos(angle)[:, None, :]
    sine = jnp.sin(angle)[:, None, :]
    first = shaped[:, :, :half]
    second = shaped[:, :, half:]
    turned = jnp.concatenate(
        [first * cosine - second * sine, second * cosine + first * sine], axis=2
    )
    return turned.reshape(values.shape[0], count * width)


def add_counts(earlier, later):
    return earlier + later


def local(tokens, segments, pre_gain, post_gain, w_query, w_key, w_value, w_out):
    rows = tokens.shape[0]
    whole = lax.all_gather(tokens, "head", axis=1, tiled=True)
    wide = whole.astype(jnp.float32)
    normed = (
        wide * lax.rsqrt(jnp.mean(wide * wide, axis=1, keepdims=True) + EPS) * pre_gain
    ).astype(jnp.bfloat16)
    pieces = (
        lax.all_gather(w_query, "seq", axis=0, tiled=True),
        lax.all_gather(w_key, "seq", axis=0, tiled=True),
        lax.all_gather(w_value, "seq", axis=0, tiled=True),
    )
    query, key_proj, value_proj = tuple(
        (jnp.dot(normed, piece, preferred_element_type=jnp.float32) for piece in pieces)
    )
    levels = jnp.arange(DOCS, dtype=jnp.int32)
    below = jnp.sum((levels[None, :] > segments[:, None]).astype(jnp.float32), axis=0)
    earlier = carried_in(below, "seq", add_counts, jnp.zeros((DOCS,), jnp.float32))
    starts = earlier + below
    onehot = (segments[:, None] == levels[None, :]).astype(jnp.float32)
    tok_start = jnp.sum(onehot * starts[None, :], axis=1)
    offset = lax.axis_index("seq") * rows
    index_f = (offset + jnp.arange(rows, dtype=jnp.int32)).astype(jnp.float32)
    position = index_f - tok_start
    kv_count = w_key.shape[1] // HD
    rq = (rotate(query, position, HD) * SCALAR ** (-0.5)).astype(jnp.bfloat16)
    rk = rotate(key_proj, position, HD).astype(jnp.bfloat16)
    vb = value_proj.astype(jnp.bfloat16)
    stacked = (
        rq.reshape(rows, kv_count, GROUP, HD)
        .transpose(1, 2, 0, 3)
        .reshape(kv_count, GROUP * rows, HD)
    )
    query_start = jnp.tile(tok_start, GROUP)
    query_index = jnp.tile(index_f, GROUP)
    empty = (
        jnp.zeros((kv_count, GROUP * rows, HD), jnp.float32),
        jnp.zeros((kv_count, GROUP * rows), jnp.float32),
    )
    keys_all = lax.all_gather(rk, "seq", axis=0, tiled=True)
    values_all = lax.all_gather(vb, "seq", axis=0, tiled=True)
    count = keys_all.shape[0]
    block = 1024
    steps_total = count // block

    def compute(offset_blk, state):
        numer, denom = state
        keys_blk = lax.dynamic_slice_in_dim(keys_all, offset_blk, block, 0).reshape(
            block, kv_count, HD
        )
        values_blk = lax.dynamic_slice_in_dim(values_all, offset_blk, block, 0).reshape(
            block, kv_count, HD
        )
        key_index = (offset_blk + jnp.arange(block, dtype=jnp.int32)).astype(jnp.float32)
        scores = jnp.einsum("cqd,kcd->cqk", stacked, keys_blk, preferred_element_type=jnp.float32)
        capped = CAP * jnp.tanh(scores / CAP)
        allowed = (key_index[None, None, :] >= query_start[None, :, None]) & (
            key_index[None, None, :] <= query_index[None, :, None]
        )
        weights = jnp.where(allowed, jnp.exp(capped), 0.0)
        numer = numer + jnp.einsum(
            "cqk,kcd->cqd",
            weights.astype(jnp.bfloat16),
            values_blk,
            preferred_element_type=jnp.float32,
        )
        denom = denom + jnp.sum(weights, axis=2)
        return (numer, denom)

    def one_block(step, state):
        offset_blk = step * block
        return compute(offset_blk, state)

    numer, denom = lax.fori_loop(0, steps_total, one_block, empty)
    attn = (numer / denom[:, :, None]).reshape(kv_count, GROUP, rows, HD).transpose(2, 0, 1, 3)
    attn = attn.reshape(rows, kv_count * GROUP * HD).astype(jnp.bfloat16)
    partial_proj = jnp.dot(
        attn, lax.all_gather(w_out, "seq", axis=1, tiled=True), preferred_element_type=jnp.float32
    )
    partial_proj = lax.optimization_barrier(partial_proj.astype(jnp.bfloat16)).astype(jnp.float32)
    summed = lax.psum(partial_proj.astype(jnp.bfloat16), "head").astype(jnp.float32)
    scale = lax.rsqrt(jnp.mean(summed * summed, axis=1, keepdims=True) + EPS)
    return (wide + summed * scale * post_gain).astype(jnp.bfloat16)


def solution(mesh):
    return jax.shard_map(
        local,
        mesh=mesh,
        in_specs=(
            P("seq", "head"),
            P("seq"),
            P(),
            P(),
            P("seq", "head"),
            P("seq", "head"),
            P("seq", "head"),
            P("head", "seq"),
        ),
        out_specs=P("seq", None),
        check_vma=False,
    )
```

profile of v0, /device:TPU:29, one launch (start us, length us, event | category | flops | bytes accessed | tf_op | source)
XLA Modules:
  0.0 297.3 jit_solution(1061354986700771852)
XLA Ops:
  6.5 0.0 copy-start.4
  6.5 0.0 all-gather.8.cloned.1.call-start
  6.5 0.7 all-gather.8.cloned.1.call-update
  7.3 0.0 all-gather.10.cloned.1.call-start
  7.3 0.7 all-gather.10.cloned.1.call-update
  8.0 0.0 all-gather.14.cloned.1.call-start
  8.1 0.7 all-gather.14.cloned.1.call-update
  8.7 0.0 all-gather.12.cloned.1.call-start
  8.8 0.5 all-gather.12.cloned.1.call-update
  9.3 0.0 all-gather.16.cloned.1.call-start
  9.4 0.5 all-gather.16.cloned.1.call-update
  9.9 0.0 all-reduce.3.cloned.1.call-start
  10.0 0.8 convert_reduce_fusion
  10.8 1.3 dynamic-slice
  12.7 0.2 dynamic-update-slice
  12.9 13.5 %all-reduce = f32[64]{0:T(128)S(1)} all-reduce(f32[64]{0:T(128)S(1)} %dynamic-update-slice), channel_id=2, replica_groups=mesh['seq'=8,'head'=4] {'seq'}, use_global_device_ids=true, to_apply=%add | all-reduce | flops 64 | bytes 512
  26.5 0.1 reshape.233
  26.6 0.3 while.30
  26.8 0.8 select_reduce_fusion
  27.6 0.3 multiply_cosine_fusion
  27.9 5.4 %all-gather.8.cloned.1.call-done = bf16[256,4608]{1,0:T(8,128)(2,1)} async-done(((bf16[256,1152]{1,0:T(8,128)(2,1)}), bf16[256,4608]{1,0:T(8,128)(2,1)}) %all-gather.8.cloned.1.call-update) | async-done | bytes 2359312 | tf_op jit(solution)/shard_map/all_gather | solution.py:50
  33.4 0.0 copy-start
  33.4 2.4 fusion.14
  35.7 38.5 %all-gather.10.cloned.1.call-done = bf16[4608,128]{1,0:T(8,128)(2,1)} async-done(((bf16[576,128]{1,0:T(8,128)(2,1)}), bf16[4608,128]{1,0:T(8,128)(2,1)}) %all-gather.10.cloned.1.call-update) | async-done | bytes 1179664 | tf_op jit(solution)/shard_map/all_gather | solution.py:57
  74.2 0.0 copy-done.4
  74.2 0.0 copy-done
  74.2 2.3 convolution_bitcast_fusion.1
  76.6 0.3 fusion.25
  76.9 26.8 %all-gather.1 = bf16[2048,1,128]{0,2,1:T(8,128)(2,1)} all-gather(bf16[256,1,128]{0,2,1:T(8,128)(2,1)S(1)} %pad_maximum_fusion), channel_id=3, replica_groups=mesh['seq'=8,'head'=4] {'seq'}, dimensions={0}, use_global_device_ids=true | all-gather | bytes 589824 | tf_op jit(solution)/shard_map/all_gather | solution.py:87
  103.7 14.2 %all-gather.14.cloned.1.call-done = bf16[4608,128]{1,0:T(8,128)(2,1)} async-done(((bf16[576,128]{1,0:T(8,128)(2,1)}), bf16[4608,128]{1,0:T(8,128)(2,1)}) %all-gather.14.cloned.1.call-update) | async-done | bytes 1179664 | tf_op jit(solution)/shard_map/all_gather | solution.py:58
  118.0 2.2 convolution_convert_fusion.1
  120.2 25.8 %all_gather.34 = bf16[2048,128]{1,0:T(8,128)(2,1)S(1)} all-gather(bf16[256,128]{1,0:T(8,128)(2,1)S(1)} %convolution_convert_fusion.1), channel_id=1, replica_groups=mesh['seq'=8,'head'=4] {'seq'}, dimensions={0}, use_global_device_ids=true | all-gather | bytes 589824 | tf_op jit(solution)/shard_map/all_gather | solution.py:88
  146.0 27.0 %all-gather.12.cloned.1.call-done = bf16[4608,256]{1,0:T(8,128)(2,1)} async-done(((bf16[576,256]{1,0:T(8,128)(2,1)}), bf16[4608,256]{1,0:T(8,128)(2,1)}) %all-gather.12.cloned.1.call-update) | async-done | bytes 2359312 | tf_op jit(solution)/shard_map/all_gather | solution.py:56
  172.9 3.0 fusion.30
  176.0 0.1 copy.16
  176.1 5.0 %while.31 = (s32[]{:T(128)}, f32[1,512,128]{2,1,0:T(8,128)S(1)}, f32[1,512]{1,0:T(1,128)S(1)}, bf16[2048,128]{0,1:T(8,128)(2,1)}, bf16[1,512,128]{2,1,0:T(8,128)...) while((s32[]{:T(128)}, f32[1,512,128]{2,1,0:T(8,128)S(1)}, ...), condition=%wide.region_7.8_spmd.clone, body=%wide.region_5.7_spmd.clone.sunk | while | flops 272763392 | bytes 3311802 | solution.py:121
  176.2 1.9 fusion.47
  178.1 0.5 fusion.48
  178.7 1.9 fusion.47
  180.6 0.5 fusion.48
  181.1 0.1 divide_convert_fusion
  181.3 0.1 copy.18
  181.4 44.6 %all-gather.16.cloned.1.call-done = bf16[256,4608]{0,1:T(8,128)(2,1)} async-done(((bf16[256,576]{0,1:T(8,128)(2,1)}), bf16[256,4608]{0,1:T(8,128)(2,1)}) %all-gather.16.cloned.1.call-update) | async-done | bytes 2359312 | tf_op jit(solution)/shard_map/all_gather | solution.py:125
  226.0 0.0 copy-start.3
  226.0 3.9 %convolution_convert_fusion = bf16[256,4608]{1,0:T(8,128)(2,1)} fusion(bf16[256,256]{0,1:T(8,128)(2,1)S(1)} %bitcast.59, bf16[256,4608]{0,1:T(8,128)(2,1)} %all-gather.16.cloned.1.call-done), kind=kOutput, calls=%fused_computation.21 | convolution fusion | flops 605159424 | bytes 4849664 | tf_op jit(solution)/shard_map/dot_general | solution.py:124
  229.9 0.0 copy-start.1
  229.9 0.0 all-reduce.3.cloned.1.call-update
  230.0 55.6 %all-reduce.3.cloned.1.call-done = bf16[256,4608]{1,0:T(8,128)(2,1)} async-done(((bf16[256,4608]{1,0:T(8,128)(2,1)}), bf16[256,4608]{1,0:T(8,128)(2,1)}) %all-reduce.3.cloned.1.call-update) | async-done | bytes 2359312 | tf_op jit(solution)/shard_map/psum | solution.py:128
  285.5 0.0 copy-start.2
  285.5 2.4 fusion.12
  287.9 0.0 copy-done.3
  287.9 0.0 copy-done.1
  287.9 0.0 copy-done.2
  287.9 2.6 fusion.17
  (30 shorter events, 0.3 us)
Async XLA Ops:
  6.5 67.7 %copy-start.4 = (f32[4608]{0:T(1024)S(1)}, f32[4608]{0:T(1024)}, u32[]{:S(2)}) copy-start(f32[4608]{0:T(1024)} %param.14) | copy-start | bytes 55300
  6.5 26.8 %all-gather.8.cloned.1.call-start = ((), (), s32[]{:S(2)}) async-start(), calls=%async_computation | async-start | bytes 2949120 | tf_op jit(solution)/shard_map/all_gather | solution.py:50
  7.3 67.0 %all-gather.10.cloned.1.call-start = ((), (), s32[]{:S(2)}) async-start(), calls=%async_computation.1 | async-start | bytes 1327104 | tf_op jit(solution)/shard_map/all_gather | solution.py:57
  8.0 110.0 %all-gather.14.cloned.1.call-start = ((), (), s32[]{:S(2)}) async-start(), calls=%async_computation.3 | async-start | bytes 1327104 | tf_op jit(solution)/shard_map/all_gather | solution.py:58
  8.7 164.2 %all-gather.12.cloned.1.call-start = ((), (), s32[]{:S(2)}) async-start(), calls=%async_computation.2 | async-start | bytes 2654208 | tf_op jit(solution)/shard_map/all_gather | solution.py:56
  9.3 216.7 %all-gather.16.cloned.1.call-start = ((), (), s32[]{:S(2)}) async-start(), calls=%async_computation.4 | async-start | bytes 2654208 | tf_op jit(solution)/shard_map/all_gather | solution.py:125
  9.9 275.6 %all-reduce.3.cloned.1.call-start = ((), (), s32[]{:S(2)}) async-start(), calls=%async_computation.5 | async-start | bytes 4718592 | tf_op jit(solution)/shard_map/psum | solution.py:128
  33.4 40.9 %copy-start = (bf16[256,4608]{1,0:T(8,128)(2,1)S(1)}, bf16[256,4608]{1,0:T(8,128)(2,1)}, u32[]{:S(2)}) copy-start(bf16[256,4608]{1,0:T(8,128)(2,1)} %all-gather.8.cloned.1.call-done) | copy-start | bytes 7077892
  226.0 61.9 %copy-start.3 = (f32[4608]{0:T(1024)S(1)}, f32[4608]{0:T(1024)}, u32[]{:S(2)}) copy-start(f32[4608]{0:T(1024)} %param.15) | copy-start | bytes 55300
  229.9 58.0 %copy-start.1 = (bf16[256,4608]{1,0:T(8,128)(2,1)S(1)}, bf16[256,4608]{1,0:T(8,128)(2,1)}, u32[]{:S(2)}) copy-start(bf16[256,4608]{1,0:T(8,128)(2,1)} %all-gather.8.cloned.1.call-done) | copy-start | bytes 7077892
  285.5 2.4 copy-start.2
Sparse Core Ops, SparseCore 0:
  8.9 24.4 all-gather.7
  35.5 38.6 all-gather.9
  76.4 41.5 all-gather.13
  120.0 52.9 all-gather.11
  175.0 50.9 all-gather.15
  230.1 55.4 all-reduce.2
where the time goes:
time: 300 us; the launch traced here: 297 us
  waiting for transfers between devices  188 us (63%)
  blocking collectives  66.2 us (22%)
  matrix products  16.2 us (5%)
  between operations  14.3 us (5%)
  other arithmetic  9.87 us (3%)
    psum x1, waiting for transfers between devices, local(): lax.psum(partial_proj.astype(jnp.bfloat16), 'head').astype(jnp.float32)  55.6 us
    all_gather x1, waiting for transfers between devices, local(): lax.all_gather(w_out, 'seq', axis=1, tiled=True)  44.6 us
    all_gather x1, waiting for transfers between devices, local(): lax.all_gather(w_key, 'seq', axis=0, tiled=True)  38.5 us
    all_gather x1, waiting for transfers between devices, local(): lax.all_gather(w_query, 'seq', axis=0, tiled=True)  27 us
    all_gather x1, blocking collectives, local(): keys_all = lax.all_gather(rk, 'seq', axis=0, tiled=True)  26.8 us
    all_gather x1, blocking collectives, local(): values_all = lax.all_gather(vb, 'seq', axis=0, tiled=True)  25.8 us
    all_gather x1, waiting for transfers between devices, local(): lax.all_gather(w_value, 'seq', axis=0, tiled=True)  14.2 us
    unnamed x1, blocking collectives  13.5 us
  transfers between devices with their start and end apart: 6, of which 6 were waited for; matrix products, arithmetic and copies ran while one was open for 6% of the time, Pallas kernels for 0%

commit v1 on v0

--- a/solution.py
+++ b/solution.py
@@ -1,6 +1,10 @@
+import functools
+
 import jax
 import jax.numpy as jnp
 from jax import lax
+from jax.experimental import pallas as pl
+from jax.experimental.pallas import tpu as pltpu
 from jax.sharding import PartitionSpec as P
 
 HD = 128
@@ -130,20 +134,432 @@
     return (wide + summed * scale * post_gain).astype(jnp.bfloat16)
 
 
+MESH = pl.DeviceIdType.MESH
+BF16 = jnp.bfloat16
+F32 = jnp.float32
+
+
+def fits(mesh, tokens, w_key, w_out):
+    seq, head = mesh.shape["seq"], mesh.shape["head"]
+    width = tokens[1]
+    lanes = -(-(width // seq) // 128) * 128
+    weights = 2 * width * (w_key[1] // head) * (GROUP + 2)
+    outs = 2 * w_out[0] * lanes * seq
+    rows = tokens[0] // seq
+    rest = rows * width * (2 + 2 + 4 + 2) + tokens[0] * (w_key[1] // head) * 4
+    return (
+        seq % 2 == 0
+        and seq > 2
+        and head % 2 == 0
+        and seq % head == 0
+        and w_key[1] // head == HD
+        and (width // head) % 128 == 0
+        and weights + outs + rest < 40 * 2**20
+    )
+
+
+class Line:
+    def __init__(self, ref, recv, send, seq, down=True):
+        self.ref, self.recv, self.send, self.down = ref, recv, send, down
+        self.count = seq // 2
+        me = lax.axis_index("seq")
+        self.z, self.x = me // 2, lax.rem(me, 2)
+        self.head = lax.axis_index("head")
+        self.me = me
+
+    def copy(self, block, way):
+        target = (
+            2 * (self.z + 1) + self.x,
+            2 * (self.z - 1) + self.x,
+            2 * self.z + 1 - self.x,
+        )[way]
+        return pltpu.make_async_remote_copy(
+            src_ref=self.ref(block),
+            dst_ref=self.ref(block),
+            send_sem=self.send.at[way, block],
+            recv_sem=self.recv.at[block],
+            device_id=(target, self.head),
+            device_id_type=MESH,
+        )
+
+    def up(self, block):
+        @pl.when(self.z < self.count - 1)
+        def _():
+            self.copy(block, 0).start()
+
+    def below(self, block):
+        if self.down:
+
+            @pl.when(self.z > 0)
+            def _():
+                self.copy(block, 1).start()
+
+    def across(self, block):
+        self.copy(block, 2).start()
+
+    def wait(self, block):
+        self.copy(block, 2).wait_recv()
+
+    def step(self, k, also=None):
+        @pl.when(self.z - k >= 0)
+        def _():
+            block = 2 * (self.z - k) + self.x
+            self.wait(block)
+            self.up(block)
+            self.across(block)
+            if also is not None:
+                also(block)
+
+        if self.down:
+
+            @pl.when(self.z + k < self.count)
+            def _():
+                block = 2 * (self.z + k) + self.x
+                self.wait(block)
+                self.below(block)
+                self.across(block)
+                if also is not None:
+                    also(block)
+
+    def pairs(self, also=None):
+        for z in range(self.count):
+            block = 2 * z + 1 - self.x
+
+            def take():
+                self.wait(block)
+                if also is not None:
+                    also(block)
+
+            if self.down:
+                take()
+            else:
+                pl.when(z <= self.z)(take)
+
+    def drain(self):
+        for z in range(self.count):
+            block = 2 * z + self.x
+
+            def sent():
+                self.copy(block, 2).wait_send()
+
+            if self.down:
+                sent()
+
+                @pl.when((self.z > 0) & (z >= self.z))
+                def _():
+                    self.copy(block, 1).wait_send()
+            else:
+                pl.when(z <= self.z)(sent)
+
+            @pl.when((self.z < self.count - 1) & (z <= self.z))
+            def _():
+                self.copy(block, 0).wait_send()
+
+
+def kernel(
+    seq, heads, rows, width,
+    tok, seg_row, wq, wk, wv, wo_in, seg_col, pre, post, freq,
+    out,
+    X, XN, W, WO, SEG, KV, ATT, PR, ACC, RQ, NUM, DEN,
+    loc, x_recv, x_send, x_core, s_recv, s_send, w_recv, w_send,
+    o_recv, o_send, o_y, o_core, k_recv, k_send, a_recv, a_send, a_core,
+):
+    me, head = lax.axis_index("seq"), lax.axis_index("head")
+    z, x = me // 2, lax.rem(me, 2)
+    y, core = head // 2, lax.rem(head, 2)
+    ys, line = heads // 2, seq // 2
+    partner = 2 * y + 1 - core
+    deep = width // seq
+    cut = width // heads
+    mates = [2 * lax.rem(y + d, ys) + core for d in range(1, ys)]
+
+    moves = [
+        pltpu.make_async_copy(seg_row, SEG.at[me], loc.at[0]),
+        pltpu.make_async_copy(tok, X.at[head], loc.at[1]),
+    ]
+    mine = W.at[pl.ds(pl.multiple_of(me * deep, 16), deep)]
+    kd = wk.shape[1]
+    qd = wq.shape[1]
+    moves += [
+        pltpu.make_async_copy(wq, mine.at[:, pl.ds(0, qd)], loc.at[2]),
+        pltpu.make_async_copy(wk, mine.at[:, pl.ds(qd, kd)], loc.at[3]),
+        pltpu.make_async_copy(wv, mine.at[:, pl.ds(qd + kd, kd)], loc.at[4]),
+        pltpu.make_async_copy(wo_in, WO.at[me, head], loc.at[5]),
+    ]
+    for move in moves:
+        move.start()
+
+    barrier = pltpu.get_barrier_semaphore()
+
+    def greet(where):
+        pl.semaphore_signal(barrier, inc=1, device_id=where, device_id_type=MESH)
+
+    greet((2 * z + 1 - x, head))
+    greet((me, partner))
+    for mate in mates:
+        greet((me, mate))
+
+    @pl.when(z > 0)
+    def _():
+        greet((me - 2, head))
+
+    @pl.when(z < line - 1)
+    def _():
+        greet((me + 2, head))
+
+    ends = (z > 0).astype(jnp.int32) + (z < line - 1).astype(jnp.int32)
+    pl.semaphore_wait(barrier, 2 + len(mates) + ends)
+
+    for move in moves:
+        move.wait()
+
+    def sent_to(ref, send, recv, where):
+        return pltpu.make_async_remote_copy(
+            src_ref=ref, dst_ref=ref, send_sem=send, recv_sem=recv,
+            device_id=where, device_id_type=MESH,
+        )
+
+    def x_copy(h, to, send):
+        return sent_to(X.at[h], send, x_recv.at[h], (me, to))
+
+    def a_copy(h, to, send):
+        return sent_to(ATT.at[h], send, a_recv.at[h], (me, to))
+
+    def o_copy(b, h, to, send):
+        return sent_to(WO.at[b, h], send, o_recv.at[b, h], (me, to))
+
+    segs = Line(lambda b: SEG.at[b], s_recv, s_send, seq)
+    ws = Line(lambda b: W.at[pl.ds(pl.multiple_of(b * deep, 16), deep)], w_recv, w_send, seq)
+    kvs = Line(lambda b: KV.at[b], k_recv, k_send, seq, down=False)
+    wos = Line(lambda b: WO.at[b, head], o_recv.at[:, head], o_send, seq)
+
+    def share(b):
+        for d, mate in enumerate(mates):
+            o_copy(b, head, mate, o_y.at[d, b]).start()
+        o_copy(b, head, partner, o_core.at[b, y]).start()
+
+    def begin(stream):
+        stream.up(me)
+        stream.below(me)
+        stream.across(me)
+
+    begin(segs)
+    for d, mate in enumerate(mates):
+        x_copy(head, mate, x_send.at[d]).start()
+    x_copy(head, partner, x_core.at[y]).start()
+    begin(ws)
+    share(me)
+
+    for k in range(1, line):
+        segs.step(k)
+        ws.step(k)
+        if k == 1:
+            for mate in mates:
+                x_copy(mate, partner, x_core.at[mate // 2]).wait_recv()
+                x_copy(mate, partner, x_core.at[mate // 2]).start()
+            wos.up(me)
+            wos.below(me)
+        if k == line - 1:
+            wos.across(me)
+    for other in range(ys):
+        x_copy(2 * other + 1 - core, partner, x_core.at[other]).wait_recv()
+
+    half = rows // 2
+
+    def norm_rows(r, _):
+        at = pl.ds(pl.multiple_of(r * half, half), half)
+        total = jnp.zeros((half, 1), F32)
+        for h in range(heads):
+            wide = X[h, at, :].astype(F32)
+            total += jnp.sum(wide * wide, axis=1, keepdims=True)
+        scale = lax.rsqrt(total / width + EPS)
+        for h in range(heads):
+            XN[h, at, :] = (X[h, at, :].astype(F32) * scale * pre[h]).astype(BF16)
+        return 0
+
+    lax.fori_loop(0, 2, norm_rows, 0)
+    segs.pairs()
+    col = seg_col[...]
+    start = jnp.zeros((rows, 1), F32)
+    for j in range(seq):
+        start += jnp.sum((SEG[j, 0:1, :] < col).astype(F32), axis=1, keepdims=True)
+    index = (me * rows + lax.broadcasted_iota(jnp.int32, (rows, 1), 0)).astype(F32)
+    angle = (index - start) * freq[...]
+    cosine = jnp.cos(angle)
+    sine = jnp.sin(angle)
+    lane = lax.broadcasted_iota(jnp.int32, (rows, HD), 1)
+    sine = jnp.where(lane < HD // 2, -sine, sine)
+    ws.pairs()
+
+    ACC[...] = jnp.zeros_like(ACC)
+
+    def project(h, _):
+        part = W[pl.ds(pl.multiple_of(h * cut, 128), cut), :]
+        ACC[...] += jnp.dot(XN[h], part, preferred_element_type=F32)
+        return 0
+
+    lax.fori_loop(0, heads, project, 0)
+
+    def turn(values):
+        return values * cosine + pltpu.roll(values, HD // 2, 1) * sine
+
+    for g in range(GROUP):
+        RQ[g * rows : (g + 1) * rows, :] = (
+            turn(ACC[:, g * HD : (g + 1) * HD]) * SCALAR ** (-0.5)
+        ).astype(BF16)
+    KV[me, :, 0:HD] = turn(ACC[:, qd : qd + HD]).astype(BF16)
+    KV[me, :, HD : 2 * HD] = ACC[:, qd + kd : qd + kd + HD].astype(BF16)
+    begin(kvs)
+    for k in range(1, line):
+        kvs.step(k)
+        wos.step(k, share)
+    kvs.pairs()
+
+    start2 = jnp.concatenate([start] * GROUP, axis=0)
+    index2 = jnp.concatenate([index] * GROUP, axis=0)
+    NUM[...] = jnp.zeros_like(NUM)
+    DEN[...] = jnp.zeros_like(DEN)
+
+    def attend(j, _):
+        s = lax.dot_general(
+            RQ[...], KV[j, :, 0:HD], (((1,), (1,)), ((), ())), preferred_element_type=F32
+        )
+        at = (j * rows + lax.broadcasted_iota(jnp.int32, (1, rows), 1)).astype(F32)
+        p = jnp.where(
+            (at >= start2) & (at <= index2), jnp.exp(CAP * jnp.tanh(s * (1.0 / CAP))), 0.0
+        )
+        DEN[...] += jnp.sum(p, axis=1, keepdims=True)
+        NUM[...] += jnp.dot(p.astype(BF16), KV[j, :, HD : 2 * HD], preferred_element_type=F32)
+        return 0
+
+    lax.fori_loop(0, me + 1, attend, 0)
+    ratio = (NUM[...] / DEN[:, 0:1]).astype(BF16)
+    for g in range(GROUP):
+        ATT[head, :, g * HD : (g + 1) * HD] = ratio[g * rows : (g + 1) * rows, :]
+    for d, mate in enumerate(mates):
+        a_copy(head, mate, a_send.at[d]).start()
+    a_copy(head, partner, a_core.at[y]).start()
+
+    wos.pairs(share)
+    for mate in mates:
+        a_copy(mate, partner, a_core.at[mate // 2]).wait_recv()
+        a_copy(mate, partner, a_core.at[mate // 2]).start()
+    for b in range(seq):
+        for mate in mates:
+            o_copy(b, mate, partner, o_core.at[b, mate // 2]).wait_recv()
+            o_copy(b, mate, partner, o_core.at[b, mate // 2]).start()
+    for other in range(ys):
+        a_copy(2 * other + 1 - core, partner, a_core.at[other]).wait_recv()
+    for b in range(seq):
+        for other in range(ys):
+            o_copy(b, 2 * other + 1 - core, partner, o_core.at[b, other]).wait_recv()
+
+    def emit(b, total):
+        acc = jnp.zeros((rows, deep), F32)
+        for h in range(heads):
+            acc += (
+                jnp.dot(ATT[h], WO[b, h], preferred_element_type=F32).astype(BF16).astype(F32)
+            )
+        PR[b] = acc
+        return total + jnp.sum(acc * acc, axis=1, keepdims=True)
+
+    total = lax.fori_loop(0, seq, emit, jnp.zeros((rows, 1), F32))
+    scale = lax.rsqrt(total / width + EPS)
+    per = seq // heads
+
+    def finish(h, _):
+        wide = X[h].astype(F32)
+        parts = [PR[h * per + i] for i in range(per)]
+        proj = jnp.concatenate(parts, axis=1)
+        at = pl.ds(pl.multiple_of(h * cut, 128), cut)
+        out[:, at] = (wide + proj * scale * post[h]).astype(BF16)
+        return 0
+
+    lax.fori_loop(0, heads, finish, 0)
+
+    for stream in (segs, ws, kvs, wos):
+        stream.drain()
+    for d, mate in enumerate(mates):
+        x_copy(head, mate, x_send.at[d]).wait_send()
+        a_copy(head, mate, a_send.at[d]).wait_send()
+    for other in range(ys):
+        x_copy(2 * other + core, partner, x_core.at[other]).wait_send()
+        a_copy(2 * other + core, partner, a_core.at[other]).wait_send()
+    for b in range(seq):
+        for d, mate in enumerate(mates):
+            o_copy(b, head, mate, o_y.at[d, b]).wait_send()
+        for other in range(ys):
+            o_copy(b, 2 * other + core, partner, o_core.at[b, other]).wait_send()
+
+
+def fused(tokens, segments, pre_gain, post_gain, w_query, w_key, w_value, w_out):
+    seq, heads = lax.axis_size("seq"), lax.axis_size("head")
+    rows, cut = tokens.shape
+    width = cut * heads
+    deep = width // seq
+    qd, kd = w_query.shape[1], w_key.shape[1]
+    half = HD // 2
+    freq = 10000.0 ** (-(jnp.arange(half, dtype=F32) / half))
+    freq = jnp.concatenate([freq, freq])[None, :]
+    hbm = pl.BlockSpec(memory_space=pl.ANY)
+    vmem = pl.BlockSpec(memory_space=pltpu.VMEM)
+    dma = pltpu.SemaphoreType.DMA
+    ys = heads // 2
+    return pl.pallas_call(
+        functools.partial(kernel, seq, heads, rows, width),
+        out_shape=jax.ShapeDtypeStruct((rows, width), BF16),
+        in_specs=[hbm] * 6 + [vmem] * 4,
+        out_specs=vmem,
+        scratch_shapes=[
+            pltpu.VMEM((heads, rows, cut), BF16),
+            pltpu.VMEM((heads, rows, cut), BF16),
+            pltpu.VMEM((width, qd + 2 * kd), BF16),
+            pltpu.VMEM((seq, heads, w_out.shape[0], deep), BF16),
+            pltpu.VMEM((seq, 8, rows), jnp.int32),
+            pltpu.VMEM((seq, rows, 2 * HD), BF16),
+            pltpu.VMEM((heads, rows, GROUP * HD), BF16),
+            pltpu.VMEM((seq, rows, deep), F32),
+            pltpu.VMEM((rows, qd + 2 * kd), F32),
+            pltpu.VMEM((GROUP * rows, HD), BF16),
+            pltpu.VMEM((GROUP * rows, HD), F32),
+            pltpu.VMEM((GROUP * rows, HD), F32),
+            dma((6,)),
+            dma((heads,)), dma((max(ys - 1, 1),)), dma((ys,)),
+            dma((seq,)), dma((3, seq)),
+            dma((seq,)), dma((3, seq)),
+            dma((seq, heads)), dma((3, seq)), dma((max(ys - 1, 1), seq)), dma((seq, ys)),
+            dma((seq,)), dma((3, seq)),
+            dma((heads,)), dma((max(ys - 1, 1),)), dma((ys,)),
+        ],
+        compiler_params=pltpu.CompilerParams(
+            collective_id=0, has_side_effects=True, vmem_limit_bytes=60 * 2**20
+        ),
+    )(
+        tokens, jnp.broadcast_to(segments[None, :], (8, rows)), w_query, w_key, w_value, w_out,
+        segments[:, None], pre_gain.reshape(heads, 1, cut), post_gain.reshape(heads, 1, cut), freq,
+    )
+
+
 def solution(mesh):
-    return jax.shard_map(
-        local,
-        mesh=mesh,
-        in_specs=(
-            P("seq", "head"),
-            P("seq"),
-            P(),
-            P(),
-            P("seq", "head"),
-            P("seq", "head"),
-            P("seq", "head"),
-            P("head", "seq"),
-        ),
-        out_specs=P("seq", None),
-        check_vma=False,
-    )
+    specs = (
+        P("seq", "head"),
+        P("seq"),
+        P(),
+        P(),
+        P("seq", "head"),
+        P("seq", "head"),
+        P("seq", "head"),
+        P("head", "seq"),
+    )
+
+    def run(*args):
+        small = fits(mesh, args[0].shape, args[5].shape, args[7].shape)
+        return jax.shard_map(
+            fused if small else local,
+            mesh=mesh,
+            in_specs=specs,
+            out_specs=P("seq", None),
+            check_vma=False,
+        )(*args)
+
+    return run

time: 300 us -> 154 us (0.51)
  waiting for transfers between devices: 188 us -> 0 us
  Pallas kernels: 0 us -> 142 us
  blocking collectives: 66.2 us -> 0 us
  matrix products: 16.2 us -> 0 us
  between operations: 14.3 us -> 0.01 us
  other arithmetic: 9.87 us -> 0.61 us
  local copies, waits for them, and re-layouts: 1.85 us -> 10.5 us
    pallas_call x0 -> x1, Pallas kernels: none -> 142 us  [fused(): pl.pallas_call(functools.partial(kernel, seq, heads, rows, width), out_sh...]
    all_gather x5 -> x0, waiting for transfers between devices: 130 us -> none  [the longest x1 44.6 us: local(): lax.all_gather(w_out, 'seq', axis=1, tiled=True)]
    psum x1 -> x0, waiting for transfers between devices: 55.6 us -> none  [local(): lax.psum(partial_proj.astype(jnp.bfloat16), 'head').astype(jnp.float32)]
    all_gather x2 -> x0, blocking collectives: 52.6 us -> none  [the longest x1 26.8 us: local(): keys_all = lax.all_gather(rk, 'seq', axis=0, tiled=True)]
    dot_general x8 -> x0, matrix products: 16.2 us -> none  [the longest x3 7.5 us: local(): jnp.dot(normed, piece, preferred_element_type=jnp.float32)]
    unnamed x1 -> x0, blocking collectives: 13.5 us -> none
    reduce_sum x4 -> x0, other arithmetic: 6.28 us -> none  [the longest x1 2.36 us: local(): jnp.mean(wide * wide, axis=1, keepdims=True) + EPS]
    unnamed x13 -> x2, local copies, waits for them, and re-layouts: 1.52 us -> 5.08 us
  transfers between devices with their start and end apart: 6 -> 0, of which waited for: 6 -> 0; matrix products, arithmetic and copies ran while one was open for 6% -> 0% of each run, Pallas kernels for 0% -> 0%
where the time goes in v1:
time: 154 us; the launch traced here: 153 us
  Pallas kernels  142 us (92%)
  local copies, waits for them, and re-layouts  10.5 us (7%)
    pallas_call x1, Pallas kernels, fused(): pl.pallas_call(functools.partial(kernel, seq, heads, rows, width), out_sh...  142 us
    unnamed x2, local copies, waits for them, and re-layouts  5.08 us

profile of v1, /device:TPU:29, one launch (start us, length us, event | category | flops | bytes accessed | tf_op | source)
XLA Modules:
  0.0 153.1 jit_solution(380380279555264434)
XLA Ops:
  0.0 0.6 maximum_bitcast_fusion.freq
  0.6 1.3 broadcast_in_dim.12.seg_row
  1.9 1.3 reshape.7.pre
  3.2 1.3 reshape.8.post
  4.6 1.5 copy.11.seg_col
  6.0 1.9 %copy.10.wo_in = bf16[256,576]{1,0:T(8,128)(2,1)} copy(bf16[256,576]{0,1:T(8,128)(2,1)} %param.15) | data formatting | bytes 589824 | tf_op args[7]
  7.9 142.0 %shard_map.82 = bf16[256,4608]{1,0:T(8,128)(2,1)} custom-call(bf16[256,1152]{1,0:T(8,128)(2,1)} %tok.1, s32[8,256]{1,0:T(8,128)} %broadcast_in_dim.12.seg_row, bf16[576,256]{1,0:T(8,128)(2,1)} %wq.1, bf16[576,128]{1,0:T(8,128)(2,1)} %wk.1, bf16[576,128]{1,0:T(8,128)(2,1)} %wv.1, bf16[256,576]{1,0:T(8,128)(2,1)} %copy.10.wo_in, s32[256,1]{1,0:T(8,128)} %copy.11.seg_col, ...), custom_call_target="tpu_custom_call" | custom-call | tf_op jit(solution)/shard_map/pallas_call | solution.py:508
  149.9 3.2 %copy.13 = bf16[256,4608]{1,0:T(8,128)(2,1)} copy(bf16[256,4608]{1,0:T(8,128)(2,1)} %shard_map.82) | data formatting | bytes 4718592
  (1 shorter events, 0.0 us)

commit v2 on v1

--- a/solution.py
+++ b/solution.py
@@ -2,6 +2,7 @@
 
 import jax
 import jax.numpy as jnp
+import numpy as np
 from jax import lax
 from jax.experimental import pallas as pl
 from jax.experimental.pallas import tpu as pltpu
@@ -142,9 +143,8 @@
 def fits(mesh, tokens, w_key, w_out):
     seq, head = mesh.shape["seq"], mesh.shape["head"]
     width = tokens[1]
-    lanes = -(-(width // seq) // 128) * 128
     weights = 2 * width * (w_key[1] // head) * (GROUP + 2)
-    outs = 2 * w_out[0] * lanes * seq
+    outs = 2 * w_out[0] * width
     rows = tokens[0] // seq
     rest = rows * width * (2 + 2 + 4 + 2) + tokens[0] * (w_key[1] // head) * 4
     return (
@@ -200,29 +200,34 @@
     def wait(self, block):
         self.copy(block, 2).wait_recv()
 
-    def step(self, k, also=None):
+    def at(self, k, act):
         @pl.when(self.z - k >= 0)
         def _():
-            block = 2 * (self.z - k) + self.x
-            self.wait(block)
-            self.up(block)
-            self.across(block)
-            if also is not None:
-                also(block)
+            act(2 * (self.z - k) + self.x, self.up)
 
         if self.down:
 
             @pl.when(self.z + k < self.count)
             def _():
-                block = 2 * (self.z + k) + self.x
-                self.wait(block)
-                self.below(block)
-                self.across(block)
-                if also is not None:
-                    also(block)
-
-    def pairs(self, also=None):
-        for z in range(self.count):
+                act(2 * (self.z + k) + self.x, self.below)
+
+    def near(self, k, also):
+        def act(block, onward):
+            self.wait(block)
+            onward(block)
+            also(block)
+
+        self.at(k, act)
+
+    def far(self, k):
+        self.at(k, lambda block, onward: self.across(block))
+
+    def step(self, k):
+        self.near(k, self.across)
+
+    def pairs(self, also=None, first=0, last=None):
+        for away in range(first, self.count if last is None else last):
+            z = lax.rem(self.z + away, self.count)
             block = 2 * z + 1 - self.x
 
             def take():
@@ -258,9 +263,9 @@
 
 def kernel(
     seq, heads, rows, width,
-    tok, seg_row, wq, wk, wv, wo_in, seg_col, pre, post, freq,
+    tok, seg_row, wq, wk, wv, wo_in, pre_in, post_in, freq_in,
     out,
-    X, XN, W, WO, SEG, KV, ATT, PR, ACC, RQ, NUM, DEN,
+    X, XN, W, WO, SEG, KV, ATT, PR, ACC, RQ, NUM, DEN, pre, post, freq,
     loc, x_recv, x_send, x_core, s_recv, s_send, w_recv, w_send,
     o_recv, o_send, o_y, o_core, k_recv, k_send, a_recv, a_send, a_core,
 ):
@@ -284,8 +289,17 @@
         pltpu.make_async_copy(wq, mine.at[:, pl.ds(0, qd)], loc.at[2]),
         pltpu.make_async_copy(wk, mine.at[:, pl.ds(qd, kd)], loc.at[3]),
         pltpu.make_async_copy(wv, mine.at[:, pl.ds(qd + kd, kd)], loc.at[4]),
-        pltpu.make_async_copy(wo_in, WO.at[me, head], loc.at[5]),
+        pltpu.make_async_copy(
+            wo_in, WO.at[head, pl.ds(pl.multiple_of(me * deep, 16), deep)], loc.at[5]
+        ),
     ]
+    small = [
+        pltpu.make_async_copy(pre_in, pre, loc.at[6]),
+        pltpu.make_async_copy(post_in, post, loc.at[7]),
+        pltpu.make_async_copy(freq_in, freq, loc.at[8]),
+    ]
+    for move in small:
+        move.start()
     for move in moves:
         move.start()
 
@@ -325,13 +339,16 @@
     def a_copy(h, to, send):
         return sent_to(ATT.at[h], send, a_recv.at[h], (me, to))
 
+    def o_block(b, h):
+        return WO.at[h, pl.ds(pl.multiple_of(b * deep, 16), deep)]
+
     def o_copy(b, h, to, send):
-        return sent_to(WO.at[b, h], send, o_recv.at[b, h], (me, to))
+        return sent_to(o_block(b, h), send, o_recv.at[b, h], (me, to))
 
     segs = Line(lambda b: SEG.at[b], s_recv, s_send, seq)
     ws = Line(lambda b: W.at[pl.ds(pl.multiple_of(b * deep, 16), deep)], w_recv, w_send, seq)
     kvs = Line(lambda b: KV.at[b], k_recv, k_send, seq, down=False)
-    wos = Line(lambda b: WO.at[b, head], o_recv.at[:, head], o_send, seq)
+    wos = Line(lambda b: o_block(b, head), o_recv.at[:, head], o_send, seq)
 
     def share(b):
         for d, mate in enumerate(mates):
@@ -350,17 +367,24 @@
     begin(ws)
     share(me)
 
-    for k in range(1, line):
-        segs.step(k)
-        ws.step(k)
-        if k == 1:
-            for mate in mates:
-                x_copy(mate, partner, x_core.at[mate // 2]).wait_recv()
-                x_copy(mate, partner, x_core.at[mate // 2]).start()
+    def onset(k):
+        @pl.when(z == k)
+        def _():
             wos.up(me)
+
+        @pl.when(line - 1 - z == k)
+        def _():
             wos.below(me)
-        if k == line - 1:
-            wos.across(me)
+
+    onset(0)
+    for move in small:
+        move.wait()
+    for mate in mates:
+        x_copy(mate, partner, x_core.at[mate // 2]).wait_recv()
+        x_copy(mate, partner, x_core.at[mate // 2]).start()
+    segs.step(1)
+    ws.step(1)
+    onset(1)
     for other in range(ys):
         x_copy(2 * other + 1 - core, partner, x_core.at[other]).wait_recv()
 
@@ -374,21 +398,29 @@
             total += jnp.sum(wide * wide, axis=1, keepdims=True)
         scale = lax.rsqrt(total / width + EPS)
         for h in range(heads):
-            XN[h, at, :] = (X[h, at, :].astype(F32) * scale * pre[h]).astype(BF16)
+            gain = pre[0:1, h * cut : (h + 1) * cut]
+            XN[h, at, :] = (X[h, at, :].astype(F32) * scale * gain).astype(BF16)
         return 0
 
     lax.fori_loop(0, 2, norm_rows, 0)
+    for k in range(2, line):
+        segs.step(k)
+        ws.step(k)
+        onset(k)
+    wos.across(me)
     segs.pairs()
-    col = seg_col[...]
+    own = jnp.broadcast_to(SEG[me].astype(F32), (HD, rows))
+    col = jnp.transpose(own)[:, 0:1]
     start = jnp.zeros((rows, 1), F32)
     for j in range(seq):
-        start += jnp.sum((SEG[j, 0:1, :] < col).astype(F32), axis=1, keepdims=True)
+        start += jnp.sum((SEG[j].astype(F32) < col).astype(F32), axis=1, keepdims=True)
     index = (me * rows + lax.broadcasted_iota(jnp.int32, (rows, 1), 0)).astype(F32)
     angle = (index - start) * freq[...]
     cosine = jnp.cos(angle)
     sine = jnp.sin(angle)
     lane = lax.broadcasted_iota(jnp.int32, (rows, HD), 1)
     sine = jnp.where(lane < HD // 2, -sine, sine)
+    wos.near(1, share)
     ws.pairs()
 
     ACC[...] = jnp.zeros_like(ACC)
@@ -410,9 +442,12 @@
     KV[me, :, 0:HD] = turn(ACC[:, qd : qd + HD]).astype(BF16)
     KV[me, :, HD : 2 * HD] = ACC[:, qd + kd : qd + kd + HD].astype(BF16)
     begin(kvs)
+    wos.pairs(share, 0, 1)
     for k in range(1, line):
+        if k + 1 < line:
+            wos.near(k + 1, share)
         kvs.step(k)
-        wos.step(k, share)
+        wos.far(k)
     kvs.pairs()
 
     start2 = jnp.concatenate([start] * GROUP, axis=0)
@@ -440,7 +475,7 @@
         a_copy(head, mate, a_send.at[d]).start()
     a_copy(head, partner, a_core.at[y]).start()
 
-    wos.pairs(share)
+    wos.pairs(share, 1)
     for mate in mates:
         a_copy(mate, partner, a_core.at[mate // 2]).wait_recv()
         a_copy(mate, partner, a_core.at[mate // 2]).start()
@@ -454,25 +489,23 @@
         for other in range(ys):
             o_copy(b, 2 * other + 1 - core, partner, o_core.at[b, other]).wait_recv()
 
-    def emit(b, total):
-        acc = jnp.zeros((rows, deep), F32)
+    def emit(n, total):
+        acc = jnp.zeros((rows, cut), F32)
+        at = pl.ds(pl.multiple_of(n * cut, 128), cut)
         for h in range(heads):
-            acc += (
-                jnp.dot(ATT[h], WO[b, h], preferred_element_type=F32).astype(BF16).astype(F32)
+            part = lax.dot_general(
+                ATT[h], WO[h, at, :], (((1,), (1,)), ((), ())), preferred_element_type=F32
             )
-        PR[b] = acc
+            acc += part.astype(BF16).astype(F32)
+        PR[n] = acc
         return total + jnp.sum(acc * acc, axis=1, keepdims=True)
 
-    total = lax.fori_loop(0, seq, emit, jnp.zeros((rows, 1), F32))
+    total = lax.fori_loop(0, heads, emit, jnp.zeros((rows, 1), F32))
     scale = lax.rsqrt(total / width + EPS)
-    per = seq // heads
 
     def finish(h, _):
-        wide = X[h].astype(F32)
-        parts = [PR[h * per + i] for i in range(per)]
-        proj = jnp.concatenate(parts, axis=1)
         at = pl.ds(pl.multiple_of(h * cut, 128), cut)
-        out[:, at] = (wide + proj * scale * post[h]).astype(BF16)
+        out[:, at] = (X[h].astype(F32) + PR[h] * scale * post[0:1, at]).astype(BF16)
         return 0
 
     lax.fori_loop(0, heads, finish, 0)
@@ -499,8 +532,8 @@
     deep = width // seq
     qd, kd = w_query.shape[1], w_key.shape[1]
     half = HD // 2
-    freq = 10000.0 ** (-(jnp.arange(half, dtype=F32) / half))
-    freq = jnp.concatenate([freq, freq])[None, :]
+    freq = np.float32(10000.0) ** (-(np.arange(half, dtype=np.float32) / np.float32(half)))
+    freq = np.concatenate([freq, freq])[None, :].astype(np.float32)
     hbm = pl.BlockSpec(memory_space=pl.ANY)
     vmem = pl.BlockSpec(memory_space=pltpu.VMEM)
     dma = pltpu.SemaphoreType.DMA
@@ -508,22 +541,25 @@
     return pl.pallas_call(
         functools.partial(kernel, seq, heads, rows, width),
         out_shape=jax.ShapeDtypeStruct((rows, width), BF16),
-        in_specs=[hbm] * 6 + [vmem] * 4,
+        in_specs=[hbm] * 9,
         out_specs=vmem,
         scratch_shapes=[
             pltpu.VMEM((heads, rows, cut), BF16),
             pltpu.VMEM((heads, rows, cut), BF16),
             pltpu.VMEM((width, qd + 2 * kd), BF16),
-            pltpu.VMEM((seq, heads, w_out.shape[0], deep), BF16),
-            pltpu.VMEM((seq, 8, rows), jnp.int32),
+            pltpu.VMEM((heads, width, w_out.shape[0]), BF16),
+            pltpu.VMEM((seq, 1, rows), jnp.int32),
             pltpu.VMEM((seq, rows, 2 * HD), BF16),
             pltpu.VMEM((heads, rows, GROUP * HD), BF16),
-            pltpu.VMEM((seq, rows, deep), F32),
+            pltpu.VMEM((heads, rows, cut), F32),
             pltpu.VMEM((rows, qd + 2 * kd), F32),
             pltpu.VMEM((GROUP * rows, HD), BF16),
             pltpu.VMEM((GROUP * rows, HD), F32),
             pltpu.VMEM((GROUP * rows, HD), F32),
-            dma((6,)),
+            pltpu.VMEM((1, width), F32),
+            pltpu.VMEM((1, width), F32),
+            pltpu.VMEM((1, HD), F32),
+            dma((9,)),
             dma((heads,)), dma((max(ys - 1, 1),)), dma((ys,)),
             dma((seq,)), dma((3, seq)),
             dma((seq,)), dma((3, seq)),
@@ -535,8 +571,8 @@
             collective_id=0, has_side_effects=True, vmem_limit_bytes=60 * 2**20
         ),
     )(
-        tokens, jnp.broadcast_to(segments[None, :], (8, rows)), w_query, w_key, w_value, w_out,
-        segments[:, None], pre_gain.reshape(heads, 1, cut), post_gain.reshape(heads, 1, cut), freq,
+        tokens, segments[None, :], w_query, w_key, w_value, w_out.T,
+        pre_gain[None, :], post_gain[None, :], freq,
     )
 
 

time: 154 us -> 125 us (0.81)
  Pallas kernels: 142 us -> 119 us
  local copies, waits for them, and re-layouts: 10.5 us -> 5.9 us
    pallas_call x1, Pallas kernels: 142 us -> 119 us  [fused(): pl.pallas_call(functools.partial(kernel, seq, heads, rows, width), out_sh...]
    reshape x2 -> x0, local copies, waits for them, and re-layouts: 2.68 us -> none  [the longest x1 1.34 us: fused(): post_gain.reshape(heads, 1, cut)]
    unnamed x2 -> x1, local copies, waits for them, and re-layouts: 5.08 us -> 3.22 us
where the time goes in v2:
time: 125 us
  Pallas kernels  119 us (95%)
  local copies, waits for them, and re-layouts  5.9 us (5%)
    pallas_call x1, Pallas kernels, fused(): pl.pallas_call(functools.partial(kernel, seq, heads, rows, width), out_sh...  119 us
    unnamed x1, local copies, waits for them, and re-layouts  3.22 us

profile of v2, /device:TPU:29, one launch (start us, length us, event | category | flops | bytes accessed | tf_op | source)
XLA Modules:
  0.0 125.2 jit_solution(17832030488646880695)
XLA Ops:
  0.0 1.3 %broadcast_in_dim.10.pre_in = f32[1,4608]{1,0:T(1,128)} reshape(f32[4608]{0:T(1024)} %param.11) | data formatting | bytes 36864 | tf_op jit(solution)/shard_map/broadcast_in_dim | solution.py:575
  1.3 1.3 %broadcast_in_dim.11.post_in = f32[1,4608]{1,0:T(1,128)} reshape(f32[4608]{0:T(1024)} %param.12) | data formatting | bytes 36864 | tf_op jit(solution)/shard_map/broadcast_in_dim | solution.py:575
  2.7 119.2 %shard_map.91 = bf16[256,4608]{1,0:T(8,128)(2,1)} custom-call(bf16[256,1152]{1,0:T(8,128)(2,1)} %tok.1, s32[1,256]{1,0:T(1,128)} %bitcast.3, bf16[576,256]{1,0:T(8,128)(2,1)} %wq.1, bf16[576,128]{1,0:T(8,128)(2,1)} %wk.1, bf16[576,128]{1,0:T(8,128)(2,1)} %wv.1, bf16[576,256]{1,0:T(8,128)(2,1)} %bitcast.2, f32[1,4608]{1,0:T(1,128)} %broadcast_in_dim.10.pre_in, ...), custom_call_target="tpu_custom_call" | custom-call | tf_op jit(solution)/shard_map/pallas_call | solution.py:541
  121.9 3.2 %copy.11 = bf16[256,4608]{1,0:T(8,128)(2,1)} copy(bf16[256,4608]{1,0:T(8,128)(2,1)} %shard_map.91) | data formatting | bytes 4718592

commit v3 on v2

--- a/solution.py
+++ b/solution.py
@@ -151,7 +151,7 @@
         seq % 2 == 0
         and seq > 2
         and head % 2 == 0
-        and seq % head == 0
+        and seq % (2 * head) == 0
         and w_key[1] // head == HD
         and (width // head) % 128 == 0
         and weights + outs + rest < 40 * 2**20
@@ -441,13 +441,15 @@
         ).astype(BF16)
     KV[me, :, 0:HD] = turn(ACC[:, qd : qd + HD]).astype(BF16)
     KV[me, :, HD : 2 * HD] = ACC[:, qd + kd : qd + kd + HD].astype(BF16)
+    wos.far(1)
     begin(kvs)
     wos.pairs(share, 0, 1)
     for k in range(1, line):
         if k + 1 < line:
             wos.near(k + 1, share)
         kvs.step(k)
-        wos.far(k)
+        if k > 1:
+            wos.far(k)
     kvs.pairs()
 
     start2 = jnp.concatenate([start] * GROUP, axis=0)
@@ -475,32 +477,61 @@
         a_copy(head, mate, a_send.at[d]).start()
     a_copy(head, partner, a_core.at[y]).start()
 
-    wos.pairs(share, 1)
+    group = line // heads
+    nest = z // group
+    less = jnp.minimum(nest, heads - 1 - nest)
+    low = (nest <= heads - 1 - nest).astype(jnp.int32)
+
+    def nearest(i):
+        near = (i <= 2 * less).astype(jnp.int32)
+        beside = nest + ((i + 1) // 2) * (1 - 2 * (i % 2))
+        past = low * i + (1 - low) * (heads - 1 - i)
+        return near * beside + (1 - near) * past
+
+    for i in range(heads):
+        for t in range(group):
+            there = nearest(i) * group + t
+            block = 2 * there + 1 - x
+
+            @pl.when(there != z)
+            def _():
+                wos.wait(block)
+                share(block)
+
     for mate in mates:
         a_copy(mate, partner, a_core.at[mate // 2]).wait_recv()
         a_copy(mate, partner, a_core.at[mate // 2]).start()
-    for b in range(seq):
-        for mate in mates:
-            o_copy(b, mate, partner, o_core.at[b, mate // 2]).wait_recv()
-            o_copy(b, mate, partner, o_core.at[b, mate // 2]).start()
     for other in range(ys):
         a_copy(2 * other + 1 - core, partner, a_core.at[other]).wait_recv()
-    for b in range(seq):
-        for other in range(ys):
-            o_copy(b, 2 * other + 1 - core, partner, o_core.at[b, other]).wait_recv()
-
-    def emit(n, total):
-        acc = jnp.zeros((rows, cut), F32)
+
+    total = jnp.zeros((rows, 1), F32)
+    for i in range(heads):
+        n = nearest(i)
+        for j in range(2 * group):
+            b = 2 * n * group + j
+            for mate in mates:
+                o_copy(b, mate, partner, o_core.at[b, mate // 2]).wait_recv()
+                o_copy(b, mate, partner, o_core.at[b, mate // 2]).start()
+        for j in range(2 * group):
+            b = 2 * n * group + j
+            for other in range(ys):
+                o_copy(b, 2 * other + 1 - core, partner, o_core.at[b, other]).wait_recv()
         at = pl.ds(pl.multiple_of(n * cut, 128), cut)
-        for h in range(heads):
-            part = lax.dot_general(
-                ATT[h], WO[h, at, :], (((1,), (1,)), ((), ())), preferred_element_type=F32
-            )
-            acc += part.astype(BF16).astype(F32)
-        PR[n] = acc
-        return total + jnp.sum(acc * acc, axis=1, keepdims=True)
-
-    total = lax.fori_loop(0, heads, emit, jnp.zeros((rows, 1), F32))
+
+        def emit(r, _):
+            some = pl.ds(pl.multiple_of(r * half, half), half)
+            acc = jnp.zeros((half, cut), F32)
+            for h in range(heads):
+                part = lax.dot_general(
+                    ATT[h, some, :], WO[h, at, :], (((1,), (1,)), ((), ())),
+                    preferred_element_type=F32,
+                )
+                acc += part.astype(BF16).astype(F32)
+            PR[n, some, :] = acc
+            return 0
+
+        lax.fori_loop(0, 2, emit, 0)
+        total += jnp.sum(PR[n] * PR[n], axis=1, keepdims=True)
     scale = lax.rsqrt(total / width + EPS)
 
     def finish(h, _):

time: 125 us -> 123 us (0.984)
  Pallas kernels: 119 us -> 117 us
    pallas_call x1, Pallas kernels: 119 us -> 117 us  [fused(): pl.pallas_call(functools.partial(kernel, seq, heads, rows, width), out_sh...]
where the time goes in v3:
time: 123 us
  Pallas kernels  117 us (95%)
  local copies, waits for them, and re-layouts  5.9 us (5%)
    pallas_call x1, Pallas kernels, fused(): pl.pallas_call(functools.partial(kernel, seq, heads, rows, width), out_sh...  117 us
    unnamed x1, local copies, waits for them, and re-layouts  3.22 us

profile of v3, /device:TPU:29, one launch (start us, length us, event | category | flops | bytes accessed | tf_op | source)
XLA Modules:
  0.0 122.9 jit_solution(8851430528244948746)
XLA Ops:
  0.0 1.3 %broadcast_in_dim.10.pre_in = f32[1,4608]{1,0:T(1,128)} reshape(f32[4608]{0:T(1024)} %param.11) | data formatting | bytes 36864 | tf_op jit(solution)/shard_map/broadcast_in_dim | solution.py:606
  1.3 1.3 %broadcast_in_dim.11.post_in = f32[1,4608]{1,0:T(1,128)} reshape(f32[4608]{0:T(1024)} %param.12) | data formatting | bytes 36864 | tf_op jit(solution)/shard_map/broadcast_in_dim | solution.py:606
  2.7 117.0 %shard_map.91 = bf16[256,4608]{1,0:T(8,128)(2,1)} custom-call(bf16[256,1152]{1,0:T(8,128)(2,1)} %tok.1, s32[1,256]{1,0:T(1,128)} %bitcast.3, bf16[576,256]{1,0:T(8,128)(2,1)} %wq.1, bf16[576,128]{1,0:T(8,128)(2,1)} %wk.1, bf16[576,128]{1,0:T(8,128)(2,1)} %wv.1, bf16[576,256]{1,0:T(8,128)(2,1)} %bitcast.2, f32[1,4608]{1,0:T(1,128)} %broadcast_in_dim.10.pre_in, ...), custom_call_target="tpu_custom_call" | custom-call | tf_op jit(solution)/shard_map/pallas_call | solution.py:572
  119.7 3.2 %copy.11 = bf16[256,4608]{1,0:T(8,128)(2,1)} copy(bf16[256,4608]{1,0:T(8,128)(2,1)} %shard_map.91) | data formatting | bytes 4718592
